TPU v7x, 32 devices: a whole 2x2x4 slice. The times are simulated.
32 devices in a mesh: row: 4 (over z), col: 8 (over y, x, core).
Axes of the slice: x: 2, y: 2, z: 4, core: 2. Of those that a mesh axis runs over, the one named last changes fastest.
Arguments:
- w_one: float32 [4, 8, 2, 256, 1024], P('row', 'col')
- w_two: float32 [4, 8, 2, 1024, 256], P('row', 'col')
- inputs: bfloat16 [4, 8, 3, 1024, 256], P('row', 'col')
- targets: bfloat16 [4, 8, 3, 1024, 256], P('row', 'col')
Outputs:
- output 1: float32 [4, 8, 2, 256, 1024], P('row', 'col')
- output 2: float32 [4, 8, 2, 1024, 256], P('row', 'col')
All inputs are finite; a program needn't handle non-finite values.
Results may differ from a plain program's by a relative error of at most 0.001.
Values are sent between devices in bfloat16 or wider.
A program may use at most 1 GiB of HBM per device.

v0:
```python
import functools

import jax
import jax.numpy as jnp
from jax import lax
from jax.experimental import pallas as pl
from jax.experimental.pallas import tpu as pltpu
from jax.sharding import PartitionSpec as P

LEARN_RATE = 1.5
NORM_EPS = 1e-6
GELU_C = 0.7978845608028654
GELU_K = 0.044715

STEPS = 3
LAYERS = 2
BATCH = 1024
DM = 256
DF = 1024
FB = 256
NB = DF // FB
RT = 256
NR = BATCH // RT
MESH = pl.DeviceIdType.MESH
F32 = jnp.float32
BF16 = jnp.bfloat16

SEND_ORDER = [(1, 0), (0, 0), (0, 1), (0, 2), (0, 3), (1, 1), (1, 2), (1, 3)]


def dot_nn(a, b):
    return lax.dot_general(a, b, (((1,), (0,)), ((), ())), preferred_element_type=F32)


def dot_nt(a, b):
    return lax.dot_general(a, b, (((1,), (1,)), ((), ())), preferred_element_type=F32)


def dot_tn(a, b):
    return lax.dot_general(a, b, (((0,), (0,)), ((), ())), preferred_element_type=F32)


def kernel(n_rows, n_cols, w1_hbm, w2_hbm, a_hbm, t_hbm, o1_hbm, o2_hbm,
           wgt, wlo, wire, recv, ain, tin, nlo, nf1, inv1, act, slope, acc, err, elo, dzb, macc,
           load_sem, data_sem, send_sem, recv_sem, out_sem):
    row = lax.axis_index("row")
    col = lax.axis_index("col")
    targets = (
        (row, lax.rem(col + 1, n_cols)),
        (row, lax.rem(col + n_cols - 1, n_cols)),
        (lax.rem(row + 1, n_rows), col),
        (lax.rem(row + n_rows - 1, n_rows), col),
    )

    barrier = pltpu.get_barrier_semaphore()
    for tgt in targets:
        pl.semaphore_signal(barrier, inc=1, device_id=tgt, device_id_type=MESH)

    def load_one(layer, blk):
        return pltpu.make_async_copy(
            w1_hbm.at[layer, :, pl.ds(pl.multiple_of(blk * FB, FB), FB)], wgt.at[layer, blk, 0], load_sem.at[layer, blk, 0])

    def load_two(layer, blk):
        return pltpu.make_async_copy(
            w2_hbm.at[layer, pl.ds(pl.multiple_of(blk * FB, FB), FB), :], wgt.at[layer, blk, 1], load_sem.at[layer, blk, 1])

    def store_one(layer, blk):
        return pltpu.make_async_copy(
            wgt.at[layer, blk, 0], o1_hbm.at[layer, :, pl.ds(pl.multiple_of(blk * FB, FB), FB)], out_sem.at[layer, blk, 0])

    def store_two(layer, blk):
        return pltpu.make_async_copy(
            wgt.at[layer, blk, 1], o2_hbm.at[layer, pl.ds(pl.multiple_of(blk * FB, FB), FB), :], out_sem.at[layer, blk, 1])

    def load_a(step):
        return pltpu.make_async_copy(a_hbm.at[step], ain.at[step], data_sem.at[0, step])

    def load_t(step):
        return pltpu.make_async_copy(t_hbm.at[step], tin.at[step], data_sem.at[1, step])

    load_a(0).start()
    for layer in range(LAYERS):
        for blk in range(NB):
            load_one(layer, blk).start()
            load_two(layer, blk).start()
    load_t(0).start()
    for step in range(1, STEPS):
        load_a(step).start()
        load_t(step).start()

    def send(step, slot, layer, blk):
        par = lax.rem(step, 2)
        return pltpu.make_async_remote_copy(
            src_ref=wire.at[layer, blk],
            dst_ref=recv.at[par, slot, layer, blk],
            send_sem=send_sem.at[slot, layer, blk],
            recv_sem=recv_sem.at[par, slot, layer, blk],
            device_id=targets[slot],
            device_id_type=MESH,
        )

    def start_sends(step, layer, blk):
        for slot in (2, 3, 0, 1):
            send(step, slot, layer, blk).start()

    def combine(step, layer, blk, keep_lo):
        par = lax.rem(step, 2)
        for slot in range(4):
            send(step, slot, layer, blk).wait_recv()
        for which in range(2):
            @pl.loop(0, FB, step=64)
            def _(r0):
                rows = pl.ds(pl.multiple_of(r0, 64), 64)
                tot = wgt[layer, blk, which, rows]
                for slot in range(4):
                    tot = tot + recv[par, slot, layer, blk, which, rows].astype(F32)
                tot = tot * 0.2
                wgt[layer, blk, which, rows] = tot
                if keep_lo:
                    wlo[layer, blk, which, rows] = tot.astype(BF16)

    def normalise(step, layer):
        @pl.loop(0, BATCH, step=128)
        def _(r0):
            rows = pl.ds(pl.multiple_of(r0, 128), 128)
            if layer == 0:
                x = ain[step, rows].astype(F32)
            else:
                x = acc[rows].astype(BF16).astype(F32)
            inv = lax.rsqrt(jnp.mean(x * x, axis=-1, keepdims=True) + NORM_EPS)
            n = x * inv
            nlo[layer, rows] = n.astype(BF16)
            if layer == 1:
                nf1[rows] = n
                inv1[rows] = jnp.broadcast_to(inv, (128, 128))
            acc[rows] = x

    def forward_layer(step, layer):
        normalise(step, layer)

        @pl.loop(0, NB)
        def _(blk):
            @pl.when(step == 0)
            def _():
                load_one(layer, blk).wait()
                load_two(layer, blk).wait()
                for which in range(2):
                    @pl.loop(0, FB, step=64)
                    def _(r0):
                        rows = pl.ds(pl.multiple_of(r0, 64), 64)
                        wlo[layer, blk, which, rows] = wgt[layer, blk, which, rows].astype(BF16)

            @pl.when(step > 0)
            def _():
                combine(step - 1, layer, blk, True)

            w_one = wlo[layer, blk, 0]
            w_two = wlo[layer, blk, 1]
            for r in range(NR):
                rows = pl.ds(r * RT, RT)
                z = dot_nn(nlo[layer, rows], w_one)
                zz = z * z
                th = jnp.tanh(z * (GELU_C + (GELU_C * GELU_K) * zz))
                half = 0.5 + 0.5 * th
                slope[layer, blk, rows] = half + (0.5 * z) * (1.0 - th * th) * (GELU_C + (3.0 * GELU_C * GELU_K) * zz)
                a_lo = (z * half).astype(BF16)
                act[layer, blk, rows] = a_lo
                acc[rows] = acc[rows] + dot_nn(a_lo, w_two)

    def backward_layer(step, layer, send_now):
        if layer > 0:
            @pl.loop(0, BATCH, step=128)
            def _(r0):
                rows = pl.ds(pl.multiple_of(r0, 128), 128)
                macc[rows] = jnp.zeros((128, DM), F32)

        @pl.loop(0, NB)
        def _(blk):
            @pl.when(step > 0)
            def _():
                for slot in range(4):
                    send(step - 1, slot, layer, blk).wait_send()

            g_two = dot_tn(act[layer, blk], elo[...])
            q_two = wgt[layer, blk, 1] - LEARN_RATE * g_two
            wgt[layer, blk, 1] = q_two
            wire[layer, blk, 1] = q_two.astype(BF16)
            w_one = wlo[layer, blk, 0]
            w_two = wlo[layer, blk, 1]
            for r in range(NR):
                rows = pl.ds(r * RT, RT)
                u = dot_nt(elo[rows], w_two)
                dz = (u * slope[layer, blk, rows]).astype(BF16)
                dzb[rows] = dz
                if layer > 0:
                    macc[rows] = macc[rows] + dot_nt(dz, w_one)
            g_one = dot_tn(nlo[layer], dzb[...])
            q_one = wgt[layer, blk, 0] - LEARN_RATE * g_one
            wgt[layer, blk, 0] = q_one
            wire[layer, blk, 0] = q_one.astype(BF16)
            send_now(blk)

    @pl.loop(0, STEPS)
    def _(step):
        load_a(step).wait()
        forward_layer(step, 0)
        forward_layer(step, 1)

        load_t(step).wait()

        @pl.loop(0, BATCH, step=128)
        def _(r0):
            rows = pl.ds(pl.multiple_of(r0, 128), 128)
            e = (2.0 / (BATCH * DM)) * (acc[rows].astype(BF16).astype(F32) - tin[step, rows].astype(F32))
            err[rows] = e
            elo[rows] = e.astype(BF16)

        @pl.when(step == 0)
        def _():
            pl.semaphore_wait(barrier, 4)

        def send_first(blk):
            @pl.when(blk == 0)
            def _():
                start_sends(step, 1, 0)

        backward_layer(step, 1, send_first)

        @pl.loop(0, BATCH, step=128)
        def _(r0):
            rows = pl.ds(pl.multiple_of(r0, 128), 128)
            m = macc[rows]
            n = nf1[rows]
            inv = inv1[rows, 0:1]
            e = err[rows] + inv * (m - n * jnp.mean(m * n, axis=-1, keepdims=True))
            elo[rows] = e.astype(BF16)

        backward_layer(step, 0, lambda blk: start_sends(step, 0, blk))
        for blk in range(1, NB):
            start_sends(step, 1, blk)

    for layer, blk in SEND_ORDER:
        combine(STEPS - 1, layer, blk, False)
        store_one(layer, blk).start()
        store_two(layer, blk).start()
    for layer, blk in SEND_ORDER:
        for slot in range(4):
            send(STEPS - 1, slot, layer, blk).wait_send()
        store_one(layer, blk).wait()
        store_two(layer, blk).wait()


def solution(mesh):
    n_rows = mesh.shape["row"]
    n_cols = mesh.shape["col"]

    def device_fn(w_one, w_two, inputs, targets):
        chunk = (LAYERS, NB, 2, FB, DM)
        out_one, out_two = pl.pallas_call(
            functools.partial(kernel, n_rows, n_cols),
            out_shape=[
                jax.ShapeDtypeStruct((LAYERS, DM, DF), F32),
                jax.ShapeDtypeStruct((LAYERS, DF, DM), F32),
            ],
            in_specs=[pl.BlockSpec(memory_space=pl.ANY)] * 4,
            out_specs=[pl.BlockSpec(memory_space=pl.ANY)] * 2,
            scratch_shapes=[
                pltpu.VMEM(chunk, F32),
                pltpu.VMEM(chunk, BF16),
                pltpu.VMEM(chunk, BF16),
                pltpu.VMEM((2, 4) + chunk, BF16),
                pltpu.VMEM((STEPS, BATCH, DM), BF16),
                pltpu.VMEM((STEPS, BATCH, DM), BF16),
                pltpu.VMEM((LAYERS, BATCH, DM), BF16),
                pltpu.VMEM((BATCH, DM), F32),
                pltpu.VMEM((BATCH, 128), F32),
                pltpu.VMEM((LAYERS, NB, BATCH, FB), BF16),
                pltpu.VMEM((LAYERS, NB, BATCH, FB), F32),
                pltpu.VMEM((BATCH, DM), F32),
                pltpu.VMEM((BATCH, DM), F32),
                pltpu.VMEM((BATCH, DM), BF16),
                pltpu.VMEM((BATCH, FB), BF16),
                pltpu.VMEM((BATCH, DM), F32),
                pltpu.SemaphoreType.DMA((LAYERS, NB, 2)),
                pltpu.SemaphoreType.DMA((2, STEPS)),
                pltpu.SemaphoreType.DMA((4, LAYERS, NB)),
                pltpu.SemaphoreType.DMA((2, 4, LAYERS, NB)),
                pltpu.SemaphoreType.DMA((LAYERS, NB, 2)),
            ],
            compiler_params=pltpu.CompilerParams(
                collective_id=0, has_side_effects=True, vmem_limit_bytes=66 * 1000 * 1000),
        )(w_one[0, 0], w_two[0, 0], inputs[0, 0], targets[0, 0])
        return out_one[None, None], out_two[None, None]

    grid_spec = P("row", "col")
    return jax.shard_map(device_fn, mesh=mesh, in_specs=(grid_spec,) * 4, out_specs=(grid_spec,) * 2, check_vma=False)
```

profile of v0, /device:TPU:0, one launch (start us, length us, event | category | flops | bytes accessed | tf_op | source)
XLA Modules:
  0.0 301.2 jit_solution(9670417667594365014)
XLA Ops:
  0.6 295.9 %shard_map.59 = (f32[2,256,1024]{2,1,0:T(8,128)}, f32[2,1024,256]{2,1,0:T(8,128)}) custom-call(f32[2,256,1024]{2,1,0:T(8,128)} %bitcast.6, f32[2,1024,256]{2,1,0:T(8,128)} %bitcast.7, bf16[3,1024,256]{2,1,0:T(8,128)(2,1)} %bitcast.10, bf16[3,1024,256]{2,1,0:T(8,128)(2,1)} %bitcast.11), custom_call_target="tpu_custom_call" | custom-call | tf_op jit(solution)/shard_map/pallas_call | solution.py:259
  296.6 0.0 copy-start
  296.6 3.3 %copy.8 = f32[1,1,2,256,1024]{4,3,2,1,0:T(8,128)} copy(f32[1,1,2,256,1024]{4,3,2,1,0:T(8,128)} %bitcast.9) | data formatting | bytes 4194304
  299.9 0.0 copy-done
  299.9 1.3 copy.9
Async XLA Ops:
  296.6 3.3 %copy-start = (f32[2,1024,256]{2,1,0:T(8,128)S(1)}, f32[2,1024,256]{2,1,0:T(8,128)}, u32[]{:S(2)}) copy-start(f32[2,1024,256]{2,1,0:T(8,128)} %get-tuple-element.5) | copy-start | bytes 6291460
where the time goes:
time: 301 us
  Pallas kernels  296 us (98%)
  local copies, waits for them, and re-layouts  4.63 us (2%)
    pallas_call x1, Pallas kernels, device_fn(): pl.pallas_call(functools.partial(kernel, n_rows, n_cols), out_shape=[jax....  296 us

commit v1 on v0

--- a/solution.py
+++ b/solution.py
@@ -42,18 +42,24 @@
 
 def kernel(n_rows, n_cols, w1_hbm, w2_hbm, a_hbm, t_hbm, o1_hbm, o2_hbm,
            wgt, wlo, wire, recv, ain, tin, nlo, nf1, inv1, act, slope, acc, err, elo, dzb, macc,
-           load_sem, data_sem, send_sem, recv_sem, out_sem):
+           load_sem, data_sem, send_sem, recv_sem, relay_sem, out_sem):
     row = lax.axis_index("row")
     col = lax.axis_index("col")
+    half = row // 2
+    inner = jnp.logical_and(row > 0, row < n_rows - 1)
     targets = (
-        (row, lax.rem(col + 1, n_cols)),
-        (row, lax.rem(col + n_cols - 1, n_cols)),
-        (lax.rem(row + 1, n_rows), col),
-        (lax.rem(row + n_rows - 1, n_rows), col),
+        ((row, lax.rem(col + 1, n_cols)), 0),
+        ((row, lax.rem(col + n_cols - 1, n_cols)), 1),
+        ((row + 1 - 2 * half, col), 2 + half),
+        ((row - 1 + 2 * half, col), 3 - half),
     )
+    relay_slot = 2 + half
+    relay_target = ((3 - 3 * half, col), 3 - half)
 
     barrier = pltpu.get_barrier_semaphore()
-    for tgt in targets:
+    for shift in range(1, n_rows):
+        pl.semaphore_signal(barrier, inc=1, device_id=(lax.rem(row + shift, n_rows), col), device_id_type=MESH)
+    for tgt, _ in targets[:2]:
         pl.semaphore_signal(barrier, inc=1, device_id=tgt, device_id_type=MESH)
 
     def load_one(layer, blk):
@@ -88,32 +94,75 @@
         load_a(step).start()
         load_t(step).start()
 
-    def send(step, slot, layer, blk):
-        par = lax.rem(step, 2)
+    def send(step, kind, layer, blk):
+        device, slot = targets[kind]
         return pltpu.make_async_remote_copy(
             src_ref=wire.at[layer, blk],
-            dst_ref=recv.at[par, slot, layer, blk],
-            send_sem=send_sem.at[slot, layer, blk],
-            recv_sem=recv_sem.at[par, slot, layer, blk],
-            device_id=targets[slot],
+            dst_ref=recv.at[step, slot, layer, blk],
+            send_sem=send_sem.at[kind, layer, blk],
+            recv_sem=recv_sem.at[step, slot, layer, blk],
+            device_id=device,
             device_id_type=MESH,
         )
 
+    def relay(step, layer, blk):
+        device, slot = relay_target
+        return pltpu.make_async_remote_copy(
+            src_ref=recv.at[step, relay_slot, layer, blk],
+            dst_ref=recv.at[step, slot, layer, blk],
+            send_sem=relay_sem.at[layer, blk],
+            recv_sem=recv_sem.at[step, slot, layer, blk],
+            device_id=device,
+            device_id_type=MESH,
+        )
+
+    def arrival(step, slot, layer, blk):
+        return pltpu.make_async_remote_copy(
+            src_ref=wire.at[layer, blk],
+            dst_ref=recv.at[step, slot, layer, blk],
+            send_sem=send_sem.at[0, layer, blk],
+            recv_sem=recv_sem.at[step, slot, layer, blk],
+            device_id=targets[0][0],
+            device_id_type=MESH,
+        )
+
     def start_sends(step, layer, blk):
-        for slot in (2, 3, 0, 1):
-            send(step, slot, layer, blk).start()
+        for kind in (2, 0, 1):
+            send(step, kind, layer, blk).start()
+
+    def start_outward(step):
+        @pl.when(inner)
+        def _():
+            @pl.when(step > 0)
+            def _():
+                for layer, blk in SEND_ORDER:
+                    relay(step - 1, layer, blk).wait_send()
+            for layer, blk in SEND_ORDER:
+                send(step, 3, layer, blk).start()
+
+    def wait_sends(step, layer, blk):
+        for kind in range(3):
+            send(step, kind, layer, blk).wait_send()
+
+        @pl.when(inner)
+        def _():
+            send(step, 3, layer, blk).wait_send()
 
     def combine(step, layer, blk, keep_lo):
-        par = lax.rem(step, 2)
-        for slot in range(4):
-            send(step, slot, layer, blk).wait_recv()
+        arrival(step, relay_slot, layer, blk).wait_recv()
+
+        @pl.when(inner)
+        def _():
+            relay(step, layer, blk).start()
+        for slot in (0, 1, 5 - relay_slot):
+            arrival(step, slot, layer, blk).wait_recv()
         for which in range(2):
             @pl.loop(0, FB, step=64)
             def _(r0):
                 rows = pl.ds(pl.multiple_of(r0, 64), 64)
                 tot = wgt[layer, blk, which, rows]
                 for slot in range(4):
-                    tot = tot + recv[par, slot, layer, blk, which, rows].astype(F32)
+                    tot = tot + recv[step, slot, layer, blk, which, rows].astype(F32)
                 tot = tot * 0.2
                 wgt[layer, blk, which, rows] = tot
                 if keep_lo:
@@ -178,8 +227,7 @@
         def _(blk):
             @pl.when(step > 0)
             def _():
-                for slot in range(4):
-                    send(step - 1, slot, layer, blk).wait_send()
+                wait_sends(step - 1, layer, blk)
 
             g_two = dot_tn(act[layer, blk], elo[...])
             q_two = wgt[layer, blk, 1] - LEARN_RATE * g_two
@@ -200,6 +248,8 @@
             wire[layer, blk, 0] = q_one.astype(BF16)
             send_now(blk)
 
+    pl.semaphore_wait(barrier, n_rows + 1)
+
     @pl.loop(0, STEPS)
     def _(step):
         load_a(step).wait()
@@ -214,10 +264,6 @@
             e = (2.0 / (BATCH * DM)) * (acc[rows].astype(BF16).astype(F32) - tin[step, rows].astype(F32))
             err[rows] = e
             elo[rows] = e.astype(BF16)
-
-        @pl.when(step == 0)
-        def _():
-            pl.semaphore_wait(barrier, 4)
 
         def send_first(blk):
             @pl.when(blk == 0)
@@ -238,14 +284,18 @@
         backward_layer(step, 0, lambda blk: start_sends(step, 0, blk))
         for blk in range(1, NB):
             start_sends(step, 1, blk)
+        start_outward(step)
 
     for layer, blk in SEND_ORDER:
         combine(STEPS - 1, layer, blk, False)
         store_one(layer, blk).start()
         store_two(layer, blk).start()
     for layer, blk in SEND_ORDER:
-        for slot in range(4):
-            send(STEPS - 1, slot, layer, blk).wait_send()
+        wait_sends(STEPS - 1, layer, blk)
+
+        @pl.when(inner)
+        def _():
+            relay(STEPS - 1, layer, blk).wait_send()
         store_one(layer, blk).wait()
         store_two(layer, blk).wait()
 
@@ -268,7 +318,7 @@
                 pltpu.VMEM(chunk, F32),
                 pltpu.VMEM(chunk, BF16),
                 pltpu.VMEM(chunk, BF16),
-                pltpu.VMEM((2, 4) + chunk, BF16),
+                pltpu.VMEM((STEPS, 4) + chunk, BF16),
                 pltpu.VMEM((STEPS, BATCH, DM), BF16),
                 pltpu.VMEM((STEPS, BATCH, DM), BF16),
                 pltpu.VMEM((LAYERS, BATCH, DM), BF16),
@@ -284,7 +334,8 @@
                 pltpu.SemaphoreType.DMA((LAYERS, NB, 2)),
                 pltpu.SemaphoreType.DMA((2, STEPS)),
                 pltpu.SemaphoreType.DMA((4, LAYERS, NB)),
-                pltpu.SemaphoreType.DMA((2, 4, LAYERS, NB)),
+                pltpu.SemaphoreType.DMA((STEPS, 4, LAYERS, NB)),
+                pltpu.SemaphoreType.DMA((LAYERS, NB)),
                 pltpu.SemaphoreType.DMA((LAYERS, NB, 2)),
             ],
             compiler_params=pltpu.CompilerParams(

time: 301 us -> 310 us (1.030)
  Pallas kernels: 296 us -> 304 us
    pallas_call x1, Pallas kernels: 296 us -> 304 us  [device_fn(): pl.pallas_call(functools.partial(kernel, n_rows, n_cols), out_shape=[jax....]
where the time goes in v1:
time: 310 us
  Pallas kernels  304 us (98%)
  local copies, waits for them, and re-layouts  4.63 us (1%)
    pallas_call x1, Pallas kernels, device_fn(): pl.pallas_call(functools.partial(kernel, n_rows, n_cols), out_shape=[jax....  304 us

profile of v1, /device:TPU:0, one launch (start us, length us, event | category | flops | bytes accessed | tf_op | source)
XLA Modules:
  0.0 309.6 jit_solution(12948426656184218598)
XLA Ops:
  0.6 304.3 %shard_map.59 = (f32[2,256,1024]{2,1,0:T(8,128)}, f32[2,1024,256]{2,1,0:T(8,128)}) custom-call(f32[2,256,1024]{2,1,0:T(8,128)} %bitcast.6, f32[2,1024,256]{2,1,0:T(8,128)} %bitcast.7, bf16[3,1024,256]{2,1,0:T(8,128)(2,1)} %bitcast.10, bf16[3,1024,256]{2,1,0:T(8,128)(2,1)} %bitcast.11), custom_call_target="tpu_custom_call" | custom-call | tf_op jit(solution)/shard_map/pallas_call | solution.py:309
  304.9 0.0 copy-start
  304.9 3.3 %copy.8 = f32[1,1,2,256,1024]{4,3,2,1,0:T(8,128)} copy(f32[1,1,2,256,1024]{4,3,2,1,0:T(8,128)} %bitcast.9) | data formatting | bytes 4194304
  308.2 0.0 copy-done
  308.3 1.3 copy.9
Async XLA Ops:
  304.9 3.3 %copy-start = (f32[2,1024,256]{2,1,0:T(8,128)S(1)}, f32[2,1024,256]{2,1,0:T(8,128)}, u32[]{:S(2)}) copy-start(f32[2,1024,256]{2,1,0:T(8,128)} %get-tuple-element.5) | copy-start | bytes 6291460

commit v2 on v1

--- a/solution.py
+++ b/solution.py
@@ -127,16 +127,19 @@
         )
 
     def start_sends(step, layer, blk):
-        for kind in (2, 0, 1):
+        send(step, 2, layer, blk).start()
+
+        @pl.when(jnp.logical_and(inner, step == 0))
+        def _():
+            send(step, 3, layer, blk).start()
+        for kind in (0, 1):
             send(step, kind, layer, blk).start()
 
     def start_outward(step):
-        @pl.when(inner)
-        def _():
-            @pl.when(step > 0)
-            def _():
-                for layer, blk in SEND_ORDER:
-                    relay(step - 1, layer, blk).wait_send()
+        @pl.when(jnp.logical_and(inner, step > 0))
+        def _():
+            for layer, blk in SEND_ORDER:
+                relay(step - 1, layer, blk).wait_send()
             for layer, blk in SEND_ORDER:
                 send(step, 3, layer, blk).start()
 
@@ -184,13 +187,12 @@
                 inv1[rows] = jnp.broadcast_to(inv, (128, 128))
             acc[rows] = x
 
-    def forward_layer(step, layer):
+    def forward_layer(step, layer, first):
         normalise(step, layer)
 
         @pl.loop(0, NB)
         def _(blk):
-            @pl.when(step == 0)
-            def _():
+            if first:
                 load_one(layer, blk).wait()
                 load_two(layer, blk).wait()
                 for which in range(2):
@@ -198,9 +200,7 @@
                     def _(r0):
                         rows = pl.ds(pl.multiple_of(r0, 64), 64)
                         wlo[layer, blk, which, rows] = wgt[layer, blk, which, rows].astype(BF16)
-
-            @pl.when(step > 0)
-            def _():
+            else:
                 combine(step - 1, layer, blk, True)
 
             w_one = wlo[layer, blk, 0]
@@ -248,14 +248,18 @@
             wire[layer, blk, 0] = q_one.astype(BF16)
             send_now(blk)
 
+    def forward(step, first):
+        load_a(step).wait()
+        with jax.named_scope("fwd0"):
+            forward_layer(step, 0, first)
+        with jax.named_scope("fwd1"):
+            forward_layer(step, 1, first)
+
+    forward(0, True)
     pl.semaphore_wait(barrier, n_rows + 1)
 
     @pl.loop(0, STEPS)
     def _(step):
-        load_a(step).wait()
-        forward_layer(step, 0)
-        forward_layer(step, 1)
-
         load_t(step).wait()
 
         @pl.loop(0, BATCH, step=128)
@@ -285,6 +289,10 @@
         for blk in range(1, NB):
             start_sends(step, 1, blk)
         start_outward(step)
+
+        @pl.when(step < STEPS - 1)
+        def _():
+            forward(step + 1, False)
 
     for layer, blk in SEND_ORDER:
         combine(STEPS - 1, layer, blk, False)

time: 310 us -> 295 us (0.952)
  Pallas kernels: 304 us -> 290 us
    pallas_call x1, Pallas kernels: 304 us -> 290 us  [device_fn(): pl.pallas_call(functools.partial(kernel, n_rows, n_cols), out_shape=[jax....]
where the time goes in v2:
time: 295 us
  Pallas kernels  290 us (98%)
  local copies, waits for them, and re-layouts  4.63 us (2%)
    pallas_call x1, Pallas kernels, device_fn(): pl.pallas_call(functools.partial(kernel, n_rows, n_cols), out_shape=[jax....  290 us

profile of v2, /device:TPU:0, one launch (start us, length us, event | category | flops | bytes accessed | tf_op | source)
XLA Modules:
  0.0 294.9 jit_solution(12176805164776640467)
XLA Ops:
  0.6 289.7 %shard_map.59 = (f32[2,256,1024]{2,1,0:T(8,128)}, f32[2,1024,256]{2,1,0:T(8,128)}) custom-call(f32[2,256,1024]{2,1,0:T(8,128)} %bitcast.6, f32[2,1024,256]{2,1,0:T(8,128)} %bitcast.7, bf16[3,1024,256]{2,1,0:T(8,128)(2,1)} %bitcast.10, bf16[3,1024,256]{2,1,0:T(8,128)(2,1)} %bitcast.11), custom_call_target="tpu_custom_call" | custom-call | tf_op jit(solution)/shard_map/pallas_call | solution.py:317
  290.3 0.0 copy-start
  290.3 3.3 %copy.8 = f32[1,1,2,256,1024]{4,3,2,1,0:T(8,128)} copy(f32[1,1,2,256,1024]{4,3,2,1,0:T(8,128)} %bitcast.9) | data formatting | bytes 4194304
  293.6 0.0 copy-done
  293.6 1.3 copy.9
Async XLA Ops:
  290.3 3.3 %copy-start = (f32[2,1024,256]{2,1,0:T(8,128)S(1)}, f32[2,1024,256]{2,1,0:T(8,128)}, u32[]{:S(2)}) copy-start(f32[2,1024,256]{2,1,0:T(8,128)} %get-tuple-element.5) | copy-start | bytes 6291460

commit v3 on v2

--- a/solution.py
+++ b/solution.py
@@ -40,9 +40,9 @@
     return lax.dot_general(a, b, (((0,), (0,)), ((), ())), preferred_element_type=F32)
 
 
-def kernel(n_rows, n_cols, w1_hbm, w2_hbm, a_hbm, t_hbm, o1_hbm, o2_hbm,
-           wgt, wlo, wire, recv, ain, tin, nlo, nf1, inv1, act, slope, acc, err, elo, dzb, macc,
-           load_sem, data_sem, send_sem, recv_sem, relay_sem, out_sem):
+def kernel(n_rows, n_cols, w1_hbm, w2_hbm, a_hbm, t_hbm, wgt,
+           wlo, wire, recv, ain, tin, nlo, nf1, inv1, act, slope, acc, err, elo, dzb, macc,
+           load_sem, data_sem, send_sem, recv_sem, relay_sem):
     row = lax.axis_index("row")
     col = lax.axis_index("col")
     half = row // 2
@@ -69,14 +69,6 @@
     def load_two(layer, blk):
         return pltpu.make_async_copy(
             w2_hbm.at[layer, pl.ds(pl.multiple_of(blk * FB, FB), FB), :], wgt.at[layer, blk, 1], load_sem.at[layer, blk, 1])
-
-    def store_one(layer, blk):
-        return pltpu.make_async_copy(
-            wgt.at[layer, blk, 0], o1_hbm.at[layer, :, pl.ds(pl.multiple_of(blk * FB, FB), FB)], out_sem.at[layer, blk, 0])
-
-    def store_two(layer, blk):
-        return pltpu.make_async_copy(
-            wgt.at[layer, blk, 1], o2_hbm.at[layer, pl.ds(pl.multiple_of(blk * FB, FB), FB), :], out_sem.at[layer, blk, 1])
 
     def load_a(step):
         return pltpu.make_async_copy(a_hbm.at[step], ain.at[step], data_sem.at[0, step])
@@ -296,16 +288,25 @@
 
     for layer, blk in SEND_ORDER:
         combine(STEPS - 1, layer, blk, False)
-        store_one(layer, blk).start()
-        store_two(layer, blk).start()
     for layer, blk in SEND_ORDER:
         wait_sends(STEPS - 1, layer, blk)
 
         @pl.when(inner)
         def _():
             relay(STEPS - 1, layer, blk).wait_send()
-        store_one(layer, blk).wait()
-        store_two(layer, blk).wait()
+
+
+def store_kernel(wgt, o1_hbm, o2_hbm, out_sem):
+    copies = []
+    for layer in range(LAYERS):
+        for blk in range(NB):
+            span = pl.ds(blk * FB, FB)
+            copies.append(pltpu.make_async_copy(wgt.at[layer, blk, 0], o1_hbm.at[layer, :, span], out_sem.at[layer, blk, 0]))
+            copies.append(pltpu.make_async_copy(wgt.at[layer, blk, 1], o2_hbm.at[layer, span, :], out_sem.at[layer, blk, 1]))
+    for copy in copies:
+        copy.start()
+    for copy in copies:
+        copy.wait()
 
 
 def solution(mesh):
@@ -314,16 +315,12 @@
 
     def device_fn(w_one, w_two, inputs, targets):
         chunk = (LAYERS, NB, 2, FB, DM)
-        out_one, out_two = pl.pallas_call(
+        weights = pl.pallas_call(
             functools.partial(kernel, n_rows, n_cols),
-            out_shape=[
-                jax.ShapeDtypeStruct((LAYERS, DM, DF), F32),
-                jax.ShapeDtypeStruct((LAYERS, DF, DM), F32),
-            ],
+            out_shape=pltpu.VMEM(chunk, F32),
             in_specs=[pl.BlockSpec(memory_space=pl.ANY)] * 4,
-            out_specs=[pl.BlockSpec(memory_space=pl.ANY)] * 2,
+            out_specs=pl.BlockSpec(memory_space=pltpu.VMEM),
             scratch_shapes=[
-                pltpu.VMEM(chunk, F32),
                 pltpu.VMEM(chunk, BF16),
                 pltpu.VMEM(chunk, BF16),
                 pltpu.VMEM((STEPS, 4) + chunk, BF16),
@@ -344,11 +341,21 @@
                 pltpu.SemaphoreType.DMA((4, LAYERS, NB)),
                 pltpu.SemaphoreType.DMA((STEPS, 4, LAYERS, NB)),
                 pltpu.SemaphoreType.DMA((LAYERS, NB)),
-                pltpu.SemaphoreType.DMA((LAYERS, NB, 2)),
             ],
             compiler_params=pltpu.CompilerParams(
-                collective_id=0, has_side_effects=True, vmem_limit_bytes=66 * 1000 * 1000),
+                collective_id=0, has_side_effects=True, vmem_limit_bytes=58 * 2**20),
         )(w_one[0, 0], w_two[0, 0], inputs[0, 0], targets[0, 0])
+        out_one, out_two = pl.pallas_call(
+            store_kernel,
+            out_shape=[
+                jax.ShapeDtypeStruct((LAYERS, DM, DF), F32),
+                jax.ShapeDtypeStruct((LAYERS, DF, DM), F32),
+            ],
+            in_specs=[pl.BlockSpec(memory_space=pltpu.VMEM)],
+            out_specs=[pl.BlockSpec(memory_space=pl.ANY)] * 2,
+            scratch_shapes=[pltpu.SemaphoreType.DMA((LAYERS, NB, 2))],
+            compiler_params=pltpu.CompilerParams(vmem_limit_bytes=2**20),
+        )(weights)
         return out_one[None, None], out_two[None, None]
 
     grid_spec = P("row", "col")

time: 295 us -> 292 us (0.990)
  local copies, waits for them, and re-layouts: 4.63 us -> 0 us
    unnamed x4 -> x0, local copies, waits for them, and re-layouts: 4.63 us -> none
    pallas_call x1 -> x2, Pallas kernels: 290 us -> 291 us  [the longest x1 289 us: device_fn(): pl.pallas_call(functools.partial(kernel, n_rows, n_cols), out_shape=pltpu...]
where the time goes in v3:
time: 292 us; the launch traced here: 291 us
  Pallas kernels  291 us (100%)
    pallas_call x1, Pallas kernels, device_fn(): pl.pallas_call(functools.partial(kernel, n_rows, n_cols), out_shape=pltpu...  289 us

profile of v3, /device:TPU:0, one launch (start us, length us, event | category | flops | bytes accessed | tf_op | source)
XLA Modules:
  0.0 291.5 jit_solution(17602650443167670657)
XLA Ops:
  0.6 288.7 %shard_map.59.wgt = f32[2,4,2,256,256]{4,3,2,1,0:T(8,128)S(1)} custom-call(f32[2,256,1024]{2,1,0:T(8,128)} %bitcast.6, f32[2,1024,256]{2,1,0:T(8,128)} %bitcast.7, bf16[3,1024,256]{2,1,0:T(8,128)(2,1)} %bitcast.8, bf16[3,1024,256]{2,1,0:T(8,128)(2,1)} %bitcast.9), custom_call_target="tpu_custom_call" | custom-call | tf_op jit(solution)/shard_map/pallas_call | solution.py:318
  289.3 2.1 shard_map.60

commit v4 on v3

--- a/solution.py
+++ b/solution.py
@@ -25,7 +25,8 @@
 F32 = jnp.float32
 BF16 = jnp.bfloat16
 
-SEND_ORDER = [(1, 0), (0, 0), (0, 1), (0, 2), (0, 3), (1, 1), (1, 2), (1, 3)]
+EARLY = 2
+SEND_ORDER = [(1, b) for b in range(EARLY)] + [(0, b) for b in range(NB)] + [(1, b) for b in range(EARLY, NB)]
 
 
 def dot_nn(a, b):
@@ -41,7 +42,7 @@
 
 
 def kernel(n_rows, n_cols, w1_hbm, w2_hbm, a_hbm, t_hbm, wgt,
-           wlo, wire, recv, ain, tin, nlo, nf1, inv1, act, slope, acc, err, elo, dzb, macc,
+           wlo, wire, recv, ain, tin, nlo, nf1, inv1, act, pre, acc, err, elo, dzb, macc,
            load_sem, data_sem, send_sem, recv_sem, relay_sem):
     row = lax.axis_index("row")
     col = lax.axis_index("col")
@@ -56,31 +57,34 @@
     relay_slot = 2 + half
     relay_target = ((3 - 3 * half, col), 3 - half)
 
+    def load_one(layer, blk):
+        return pltpu.make_async_copy(
+            w1_hbm.at[layer, :, pl.ds(pl.multiple_of(blk * FB, FB), FB)], wgt.at[layer, blk, 0], load_sem.at[layer, blk, 0])
+
+    def load_two(layer, blk):
+        return pltpu.make_async_copy(
+            w2_hbm.at[layer, pl.ds(pl.multiple_of(blk * FB, FB), FB), :], wgt.at[layer, blk, 1], load_sem.at[layer, blk, 1])
+
+    def load_a(step):
+        return pltpu.make_async_copy(a_hbm.at[step], ain.at[step], data_sem.at[0, step])
+
+    def load_t(step):
+        return pltpu.make_async_copy(t_hbm.at[step], tin.at[step], data_sem.at[1, step])
+
+    load_a(0).start()
+    for blk in range(NB):
+        load_one(0, blk).start()
+        load_two(0, blk).start()
+
     barrier = pltpu.get_barrier_semaphore()
     for shift in range(1, n_rows):
         pl.semaphore_signal(barrier, inc=1, device_id=(lax.rem(row + shift, n_rows), col), device_id_type=MESH)
     for tgt, _ in targets[:2]:
         pl.semaphore_signal(barrier, inc=1, device_id=tgt, device_id_type=MESH)
 
-    def load_one(layer, blk):
-        return pltpu.make_async_copy(
-            w1_hbm.at[layer, :, pl.ds(pl.multiple_of(blk * FB, FB), FB)], wgt.at[layer, blk, 0], load_sem.at[layer, blk, 0])
-
-    def load_two(layer, blk):
-        return pltpu.make_async_copy(
-            w2_hbm.at[layer, pl.ds(pl.multiple_of(blk * FB, FB), FB), :], wgt.at[layer, blk, 1], load_sem.at[layer, blk, 1])
-
-    def load_a(step):
-        return pltpu.make_async_copy(a_hbm.at[step], ain.at[step], data_sem.at[0, step])
-
-    def load_t(step):
-        return pltpu.make_async_copy(t_hbm.at[step], tin.at[step], data_sem.at[1, step])
-
-    load_a(0).start()
-    for layer in range(LAYERS):
-        for blk in range(NB):
-            load_one(layer, blk).start()
-            load_two(layer, blk).start()
+    for blk in range(NB):
+        load_one(1, blk).start()
+        load_two(1, blk).start()
     load_t(0).start()
     for step in range(1, STEPS):
         load_a(step).start()
@@ -164,9 +168,8 @@
                     wlo[layer, blk, which, rows] = tot.astype(BF16)
 
     def normalise(step, layer):
-        @pl.loop(0, BATCH, step=128)
-        def _(r0):
-            rows = pl.ds(pl.multiple_of(r0, 128), 128)
+        for r0 in range(0, BATCH, 128):
+            rows = pl.ds(r0, 128)
             if layer == 0:
                 x = ain[step, rows].astype(F32)
             else:
@@ -188,9 +191,8 @@
                 load_one(layer, blk).wait()
                 load_two(layer, blk).wait()
                 for which in range(2):
-                    @pl.loop(0, FB, step=64)
-                    def _(r0):
-                        rows = pl.ds(pl.multiple_of(r0, 64), 64)
+                    for r0 in range(0, FB, 64):
+                        rows = pl.ds(r0, 64)
                         wlo[layer, blk, which, rows] = wgt[layer, blk, which, rows].astype(BF16)
             else:
                 combine(step - 1, layer, blk, True)
@@ -200,11 +202,9 @@
             for r in range(NR):
                 rows = pl.ds(r * RT, RT)
                 z = dot_nn(nlo[layer, rows], w_one)
-                zz = z * z
-                th = jnp.tanh(z * (GELU_C + (GELU_C * GELU_K) * zz))
-                half = 0.5 + 0.5 * th
-                slope[layer, blk, rows] = half + (0.5 * z) * (1.0 - th * th) * (GELU_C + (3.0 * GELU_C * GELU_K) * zz)
-                a_lo = (z * half).astype(BF16)
+                pre[layer, blk, rows] = z
+                th = jnp.tanh(z * (GELU_C + (GELU_C * GELU_K) * (z * z)))
+                a_lo = (z * (0.5 + 0.5 * th)).astype(BF16)
                 act[layer, blk, rows] = a_lo
                 acc[rows] = acc[rows] + dot_nn(a_lo, w_two)
 
@@ -230,7 +230,11 @@
             for r in range(NR):
                 rows = pl.ds(r * RT, RT)
                 u = dot_nt(elo[rows], w_two)
-                dz = (u * slope[layer, blk, rows]).astype(BF16)
+                z = pre[layer, blk, rows]
+                zz = z * z
+                th = jnp.tanh(z * (GELU_C + (GELU_C * GELU_K) * zz))
+                slope = (0.5 + 0.5 * th) * (1.0 + (z * (1.0 - th)) * (GELU_C + (3.0 * GELU_C * GELU_K) * zz))
+                dz = (u * slope).astype(BF16)
                 dzb[rows] = dz
                 if layer > 0:
                     macc[rows] = macc[rows] + dot_nt(dz, w_one)
@@ -262,9 +266,9 @@
             elo[rows] = e.astype(BF16)
 
         def send_first(blk):
-            @pl.when(blk == 0)
+            @pl.when(blk < EARLY)
             def _():
-                start_sends(step, 1, 0)
+                start_sends(step, 1, blk)
 
         backward_layer(step, 1, send_first)
 
@@ -278,7 +282,7 @@
             elo[rows] = e.astype(BF16)
 
         backward_layer(step, 0, lambda blk: start_sends(step, 0, blk))
-        for blk in range(1, NB):
+        for blk in range(EARLY, NB):
             start_sends(step, 1, blk)
         start_outward(step)
 

time: 292 us -> 288 us (0.986)
  Pallas kernels: 291 us -> 287 us
    pallas_call x1, Pallas kernels: 289 us -> 285 us  [device_fn(): pl.pallas_call(functools.partial(kernel, n_rows, n_cols), out_shape=pltpu...]
where the time goes in v4:
time: 288 us
  Pallas kernels  287 us (100%)
    pallas_call x1, Pallas kernels, device_fn(): pl.pallas_call(functools.partial(kernel, n_rows, n_cols), out_shape=pltpu...  285 us

profile of v4, /device:TPU:0, one launch (start us, length us, event | category | flops | bytes accessed | tf_op | source)
XLA Modules:
  0.0 287.5 jit_solution(16004754507974973945)
XLA Ops:
  0.6 284.7 %shard_map.59.wgt = f32[2,4,2,256,256]{4,3,2,1,0:T(8,128)S(1)} custom-call(f32[2,256,1024]{2,1,0:T(8,128)} %bitcast.6, f32[2,1024,256]{2,1,0:T(8,128)} %bitcast.7, bf16[3,1024,256]{2,1,0:T(8,128)(2,1)} %bitcast.8, bf16[3,1024,256]{2,1,0:T(8,128)(2,1)} %bitcast.9), custom_call_target="tpu_custom_call" | custom-call | tf_op jit(solution)/shard_map/pallas_call | solution.py:322
  285.4 2.1 shard_map.60

commit v5 on v4

--- a/solution.py
+++ b/solution.py
@@ -51,116 +51,107 @@
     targets = (
         ((row, lax.rem(col + 1, n_cols)), 0),
         ((row, lax.rem(col + n_cols - 1, n_cols)), 1),
-        ((row + 1 - 2 * half, col), 2 + half),
-        ((row - 1 + 2 * half, col), 3 - half),
+        ((row + 1 - 2 * half, col), lax.rem(row + half, 2) * -1 + 3),
+        ((row - 1 + 2 * half, col), 2),
     )
-    relay_slot = 2 + half
-    relay_target = ((3 - 3 * half, col), 3 - half)
+    relay_device = (3 - 3 * half, col)
 
     def load_one(layer, blk):
         return pltpu.make_async_copy(
-            w1_hbm.at[layer, :, pl.ds(pl.multiple_of(blk * FB, FB), FB)], wgt.at[layer, blk, 0], load_sem.at[layer, blk, 0])
+            w1_hbm.at[layer, :, pl.ds(pl.multiple_of(blk * FB, FB), FB)], wgt.at[layer, blk, 0], load_sem.at[layer, blk])
 
     def load_two(layer, blk):
         return pltpu.make_async_copy(
-            w2_hbm.at[layer, pl.ds(pl.multiple_of(blk * FB, FB), FB), :], wgt.at[layer, blk, 1], load_sem.at[layer, blk, 1])
-
-    def load_a(step):
-        return pltpu.make_async_copy(a_hbm.at[step], ain.at[step], data_sem.at[0, step])
-
-    def load_t(step):
-        return pltpu.make_async_copy(t_hbm.at[step], tin.at[step], data_sem.at[1, step])
-
-    load_a(0).start()
-    for blk in range(NB):
-        load_one(0, blk).start()
-        load_two(0, blk).start()
+            w2_hbm.at[layer, pl.ds(pl.multiple_of(blk * FB, FB), FB), :], wgt.at[layer, blk, 1], load_sem.at[layer, blk])
+
+    def loaded(layer, blk):
+        return pltpu.make_async_copy(wgt.at[layer, blk], wgt.at[layer, blk], load_sem.at[layer, blk])
+
+    def load_data(which, first, count):
+        src, dst = ((a_hbm, ain), (t_hbm, tin))[which]
+        return pltpu.make_async_copy(src.at[pl.ds(first, count)], dst.at[pl.ds(first, count)], data_sem.at[which, min(first, 1)])
+
+    load_data(0, 0, 1).start()
+
+    @pl.loop(0, LAYERS * NB)
+    def _(i):
+        load_one(i // NB, lax.rem(i, NB)).start()
+        load_two(i // NB, lax.rem(i, NB)).start()
 
     barrier = pltpu.get_barrier_semaphore()
     for shift in range(1, n_rows):
         pl.semaphore_signal(barrier, inc=1, device_id=(lax.rem(row + shift, n_rows), col), device_id_type=MESH)
     for tgt, _ in targets[:2]:
         pl.semaphore_signal(barrier, inc=1, device_id=tgt, device_id_type=MESH)
-
-    for blk in range(NB):
-        load_one(1, blk).start()
-        load_two(1, blk).start()
-    load_t(0).start()
-    for step in range(1, STEPS):
-        load_a(step).start()
-        load_t(step).start()
-
-    def send(step, kind, layer, blk):
+    load_data(1, 0, 1).start()
+    load_data(0, 1, STEPS - 1).start()
+    load_data(1, 1, STEPS - 1).start()
+
+    def remote(src, dst, sent, arrived, device):
+        return pltpu.make_async_remote_copy(
+            src_ref=src, dst_ref=dst, send_sem=sent, recv_sem=arrived, device_id=device, device_id_type=MESH)
+
+    def send(step, kind, layer, *blk):
         device, slot = targets[kind]
-        return pltpu.make_async_remote_copy(
-            src_ref=wire.at[layer, blk],
-            dst_ref=recv.at[step, slot, layer, blk],
-            send_sem=send_sem.at[kind, layer, blk],
-            recv_sem=recv_sem.at[step, slot, layer, blk],
-            device_id=device,
-            device_id_type=MESH,
-        )
+        group = slot - 2 if kind == 2 else 0
+        return remote(
+            wire.at[(layer,) + blk], recv.at[(step, slot, layer) + blk],
+            send_sem.at[kind], recv_sem.at[lax.rem(step, 2), group, layer, blk[0]], device)
 
     def relay(step, layer, blk):
-        device, slot = relay_target
-        return pltpu.make_async_remote_copy(
-            src_ref=recv.at[step, relay_slot, layer, blk],
-            dst_ref=recv.at[step, slot, layer, blk],
-            send_sem=relay_sem.at[layer, blk],
-            recv_sem=recv_sem.at[step, slot, layer, blk],
-            device_id=device,
-            device_id_type=MESH,
-        )
-
-    def arrival(step, slot, layer, blk):
-        return pltpu.make_async_remote_copy(
-            src_ref=wire.at[layer, blk],
-            dst_ref=recv.at[step, slot, layer, blk],
-            send_sem=send_sem.at[0, layer, blk],
-            recv_sem=recv_sem.at[step, slot, layer, blk],
-            device_id=targets[0][0],
-            device_id_type=MESH,
-        )
-
-    def start_sends(step, layer, blk):
-        send(step, 2, layer, blk).start()
+        return remote(
+            recv.at[step, 3, layer, blk], recv.at[step, 3, layer, blk],
+            relay_sem.at[0], recv_sem.at[lax.rem(step, 2), 1, layer, blk], relay_device)
+
+    def wait_far(step, layer, blk):
+        relay(step, layer, blk).wait_recv()
+
+    def wait_rest(step, layer, blk):
+        dst = recv.at[step, pl.ds(0, 3), layer, blk]
+        remote(dst, dst, send_sem.at[0], recv_sem.at[lax.rem(step, 2), 0, layer, blk], relay_device).wait_recv()
+
+    def wait_relays(step):
+        remote(recv.at[step, 3], recv.at[step, 3], relay_sem.at[0], recv_sem.at[0, 0, 0, 0], relay_device).wait_send()
+
+    def start_sends(step, layer, *blk):
+        send(step, 2, layer, *blk).start()
 
         @pl.when(jnp.logical_and(inner, step == 0))
         def _():
-            send(step, 3, layer, blk).start()
+            send(step, 3, layer, *blk).start()
         for kind in (0, 1):
-            send(step, kind, layer, blk).start()
+            send(step, kind, layer, *blk).start()
 
     def start_outward(step):
         @pl.when(jnp.logical_and(inner, step > 0))
         def _():
-            for layer, blk in SEND_ORDER:
-                relay(step - 1, layer, blk).wait_send()
+            wait_relays(step - 1)
             for layer, blk in SEND_ORDER:
                 send(step, 3, layer, blk).start()
 
-    def wait_sends(step, layer, blk):
+    def wait_sends():
         for kind in range(3):
-            send(step, kind, layer, blk).wait_send()
+            remote(wire, recv.at[0, 0], send_sem.at[kind], recv_sem.at[0, 0, 0, 0], relay_device).wait_send()
 
         @pl.when(inner)
         def _():
-            send(step, 3, layer, blk).wait_send()
+            remote(wire, recv.at[0, 0], send_sem.at[3], recv_sem.at[0, 0, 0, 0], relay_device).wait_send()
 
     def combine(step, layer, blk, keep_lo):
-        arrival(step, relay_slot, layer, blk).wait_recv()
+        with jax.named_scope("w_far"):
+            wait_far(step, layer, blk)
 
         @pl.when(inner)
         def _():
             relay(step, layer, blk).start()
-        for slot in (0, 1, 5 - relay_slot):
-            arrival(step, slot, layer, blk).wait_recv()
+        with jax.named_scope("w_rest"):
+            wait_rest(step, layer, blk)
         for which in range(2):
             @pl.loop(0, FB, step=64)
             def _(r0):
                 rows = pl.ds(pl.multiple_of(r0, 64), 64)
                 tot = wgt[layer, blk, which, rows]
-                for slot in range(4):
+                for slot in (0, 1, 3 - half, 2 + half):
                     tot = tot + recv[step, slot, layer, blk, which, rows].astype(F32)
                 tot = tot * 0.2
                 wgt[layer, blk, which, rows] = tot
@@ -185,11 +176,9 @@
     def forward_layer(step, layer, first):
         normalise(step, layer)
 
-        @pl.loop(0, NB)
-        def _(blk):
+        def block(blk):
             if first:
-                load_one(layer, blk).wait()
-                load_two(layer, blk).wait()
+                loaded(layer, blk).wait()
                 for which in range(2):
                     for r0 in range(0, FB, 64):
                         rows = pl.ds(r0, 64)
@@ -208,6 +197,12 @@
                 act[layer, blk, rows] = a_lo
                 acc[rows] = acc[rows] + dot_nn(a_lo, w_two)
 
+        if first:
+            for blk in range(NB):
+                block(blk)
+        else:
+            pl.loop(0, NB)(block)
+
     def backward_layer(step, layer, send_now):
         if layer > 0:
             @pl.loop(0, BATCH, step=128)
@@ -217,14 +212,11 @@
 
         @pl.loop(0, NB)
         def _(blk):
-            @pl.when(step > 0)
-            def _():
-                wait_sends(step - 1, layer, blk)
-
             g_two = dot_tn(act[layer, blk], elo[...])
             q_two = wgt[layer, blk, 1] - LEARN_RATE * g_two
             wgt[layer, blk, 1] = q_two
             wire[layer, blk, 1] = q_two.astype(BF16)
+            send_now(blk, 1)
             w_one = wlo[layer, blk, 0]
             w_two = wlo[layer, blk, 1]
             for r in range(NR):
@@ -242,21 +234,22 @@
             q_one = wgt[layer, blk, 0] - LEARN_RATE * g_one
             wgt[layer, blk, 0] = q_one
             wire[layer, blk, 0] = q_one.astype(BF16)
-            send_now(blk)
+            send_now(blk, 0)
 
     def forward(step, first):
-        load_a(step).wait()
         with jax.named_scope("fwd0"):
             forward_layer(step, 0, first)
         with jax.named_scope("fwd1"):
             forward_layer(step, 1, first)
 
+    load_data(0, 0, 1).wait()
     forward(0, True)
     pl.semaphore_wait(barrier, n_rows + 1)
 
+    load_data(1, 0, 1).wait()
+
     @pl.loop(0, STEPS)
     def _(step):
-        load_t(step).wait()
 
         @pl.loop(0, BATCH, step=128)
         def _(r0):
@@ -265,12 +258,17 @@
             err[rows] = e
             elo[rows] = e.astype(BF16)
 
-        def send_first(blk):
+        @pl.when(step > 0)
+        def _():
+            wait_sends()
+
+        def send_early(blk, which):
             @pl.when(blk < EARLY)
             def _():
-                start_sends(step, 1, blk)
-
-        backward_layer(step, 1, send_first)
+                start_sends(step, 1, blk, which)
+
+        with jax.named_scope("bwd1"):
+            backward_layer(step, 1, send_early)
 
         @pl.loop(0, BATCH, step=128)
         def _(r0):
@@ -281,10 +279,21 @@
             e = err[rows] + inv * (m - n * jnp.mean(m * n, axis=-1, keepdims=True))
             elo[rows] = e.astype(BF16)
 
-        backward_layer(step, 0, lambda blk: start_sends(step, 0, blk))
+        def send_whole(blk, which):
+            if which == 0:
+                start_sends(step, 0, blk)
+
+        with jax.named_scope("bwd0"):
+            backward_layer(step, 0, send_whole)
         for blk in range(EARLY, NB):
             start_sends(step, 1, blk)
-        start_outward(step)
+        with jax.named_scope("outward"):
+            start_outward(step)
+
+        @pl.when(step == 0)
+        def _():
+            load_data(0, 1, STEPS - 1).wait()
+            load_data(1, 1, STEPS - 1).wait()
 
         @pl.when(step < STEPS - 1)
         def _():
@@ -292,12 +301,11 @@
 
     for layer, blk in SEND_ORDER:
         combine(STEPS - 1, layer, blk, False)
-    for layer, blk in SEND_ORDER:
-        wait_sends(STEPS - 1, layer, blk)
-
-        @pl.when(inner)
-        def _():
-            relay(STEPS - 1, layer, blk).wait_send()
+    wait_sends()
+
+    @pl.when(inner)
+    def _():
+        wait_relays(STEPS - 1)
 
 
 def store_kernel(wgt, o1_hbm, o2_hbm, out_sem):
@@ -340,11 +348,11 @@
                 pltpu.VMEM((BATCH, DM), BF16),
                 pltpu.VMEM((BATCH, FB), BF16),
                 pltpu.VMEM((BATCH, DM), F32),
-                pltpu.SemaphoreType.DMA((LAYERS, NB, 2)),
-                pltpu.SemaphoreType.DMA((2, STEPS)),
-                pltpu.SemaphoreType.DMA((4, LAYERS, NB)),
-                pltpu.SemaphoreType.DMA((STEPS, 4, LAYERS, NB)),
                 pltpu.SemaphoreType.DMA((LAYERS, NB)),
+                pltpu.SemaphoreType.DMA((2, 2)),
+                pltpu.SemaphoreType.DMA((4,)),
+                pltpu.SemaphoreType.DMA((2, 2, LAYERS, NB)),
+                pltpu.SemaphoreType.DMA((1,)),
             ],
             compiler_params=pltpu.CompilerParams(
                 collective_id=0, has_side_effects=True, vmem_limit_bytes=58 * 2**20),

time: 288 us -> 284 us (0.986)
  Pallas kernels: 287 us -> 284 us
    pallas_call x1, Pallas kernels: 285 us -> 281 us  [device_fn(): pl.pallas_call(functools.partial(kernel, n_rows, n_cols), out_shape=pltpu...]
where the time goes in v5:
time: 284 us
  Pallas kernels  284 us (100%)
    pallas_call x1, Pallas kernels, device_fn(): pl.pallas_call(functools.partial(kernel, n_rows, n_cols), out_shape=pltpu...  281 us

profile of v5, /device:TPU:0, one launch (start us, length us, event | category | flops | bytes accessed | tf_op | source)
XLA Modules:
  0.0 284.2 jit_solution(524805391359893341)
XLA Ops:
  0.6 281.5 %shard_map.59.wgt = f32[2,4,2,256,256]{4,3,2,1,0:T(8,128)S(1)} custom-call(f32[2,256,1024]{2,1,0:T(8,128)} %bitcast.6, f32[2,1024,256]{2,1,0:T(8,128)} %bitcast.7, bf16[3,1024,256]{2,1,0:T(8,128)(2,1)} %bitcast.8, bf16[3,1024,256]{2,1,0:T(8,128)(2,1)} %bitcast.9), custom_call_target="tpu_custom_call" | custom-call | tf_op jit(solution)/shard_map/pallas_call | solution.py:330
  282.1 2.1 shard_map.60

commit v6 on v5

--- a/solution.py
+++ b/solution.py
@@ -21,6 +21,7 @@
 NB = DF // FB
 RT = 256
 NR = BATCH // RT
+RT1 = 256
 MESH = pl.DeviceIdType.MESH
 F32 = jnp.float32
 BF16 = jnp.bfloat16
@@ -42,7 +43,7 @@
 
 
 def kernel(n_rows, n_cols, w1_hbm, w2_hbm, a_hbm, t_hbm, wgt,
-           wlo, wire, recv, ain, tin, nlo, nf1, inv1, act, pre, acc, err, elo, dzb, macc,
+           wlo, wire, recv, ain, tin, nlo, nf1, inv1, act, acc, err, elo, dzb, macc,
            load_sem, data_sem, send_sem, recv_sem, relay_sem):
     row = lax.axis_index("row")
     col = lax.axis_index("col")
@@ -113,8 +114,13 @@
     def wait_relays(step):
         remote(recv.at[step, 3], recv.at[step, 3], relay_sem.at[0], recv_sem.at[0, 0, 0, 0], relay_device).wait_send()
 
-    def start_sends(step, layer, *blk):
-        send(step, 2, layer, *blk).start()
+    def start_sends(step, layer, *blk, hold=False):
+        if hold:
+            @pl.when(jnp.logical_not(jnp.logical_and(inner, step == STEPS - 1)))
+            def _():
+                send(step, 2, layer, *blk).start()
+        else:
+            send(step, 2, layer, *blk).start()
 
         @pl.when(jnp.logical_and(inner, step == 0))
         def _():
@@ -137,13 +143,17 @@
         def _():
             remote(wire, recv.at[0, 0], send_sem.at[3], recv_sem.at[0, 0, 0, 0], relay_device).wait_send()
 
-    def combine(step, layer, blk, keep_lo):
+    def combine(step, layer, blk, keep_lo, held_back=False):
         with jax.named_scope("w_far"):
             wait_far(step, layer, blk)
 
         @pl.when(inner)
         def _():
             relay(step, layer, blk).start()
+        if held_back:
+            @pl.when(inner)
+            def _():
+                send(step, 2, layer, blk).start()
         with jax.named_scope("w_rest"):
             wait_rest(step, layer, blk)
         for which in range(2):
@@ -158,50 +168,63 @@
                 if keep_lo:
                     wlo[layer, blk, which, rows] = tot.astype(BF16)
 
-    def normalise(step, layer):
+    def normalise(layer, rows, x):
+        inv = lax.rsqrt(jnp.mean(x * x, axis=-1, keepdims=True) + NORM_EPS)
+        n = x * inv
+        nlo[layer, rows] = n.astype(BF16)
+        if layer == 1:
+            nf1[rows] = n
+            inv1[rows] = jnp.broadcast_to(inv, (x.shape[0], 128))
+
+    def activation(layer, blk, rows):
+        z = dot_nn(nlo[layer, rows], wlo[layer, blk, 0])
+        th = jnp.tanh(z * (GELU_C + (GELU_C * GELU_K) * (z * z)))
+        a_lo = (z * (0.5 + 0.5 * th)).astype(BF16)
+        act[layer, blk, rows] = a_lo
+        return a_lo
+
+    def error(step, rows, total):
+        e = (2.0 / (BATCH * DM)) * (total.astype(BF16).astype(F32) - tin[step, rows].astype(F32))
+        err[rows] = e
+        elo[rows] = e.astype(BF16)
+
+    def first_forward():
+        load_data(0, 0, 1).wait()
+        for layer in range(LAYERS):
+            if layer == LAYERS - 1:
+                load_data(1, 0, 1).wait()
+            for r in range(BATCH // RT1):
+                rows = pl.ds(r * RT1, RT1)
+                if layer == 0:
+                    total = ain[0, rows].astype(F32)
+                    normalise(layer, rows, total)
+                else:
+                    total = acc[rows]
+                for blk in range(NB):
+                    if r == 0:
+                        loaded(layer, blk).wait()
+                        wlo[layer, blk] = wgt[layer, blk].astype(BF16)
+                    total = total + dot_nn(activation(layer, blk, rows), wlo[layer, blk, 1])
+                if layer == 0:
+                    total = total.astype(BF16).astype(F32)
+                    normalise(1, rows, total)
+                    acc[rows] = total
+                else:
+                    error(0, rows, total)
+
+    def forward_layer(step, layer):
         for r0 in range(0, BATCH, 128):
             rows = pl.ds(r0, 128)
-            if layer == 0:
-                x = ain[step, rows].astype(F32)
-            else:
-                x = acc[rows].astype(BF16).astype(F32)
-            inv = lax.rsqrt(jnp.mean(x * x, axis=-1, keepdims=True) + NORM_EPS)
-            n = x * inv
-            nlo[layer, rows] = n.astype(BF16)
-            if layer == 1:
-                nf1[rows] = n
-                inv1[rows] = jnp.broadcast_to(inv, (128, 128))
+            x = ain[step, rows].astype(F32) if layer == 0 else acc[rows].astype(BF16).astype(F32)
+            normalise(layer, rows, x)
             acc[rows] = x
 
-    def forward_layer(step, layer, first):
-        normalise(step, layer)
-
-        def block(blk):
-            if first:
-                loaded(layer, blk).wait()
-                for which in range(2):
-                    for r0 in range(0, FB, 64):
-                        rows = pl.ds(r0, 64)
-                        wlo[layer, blk, which, rows] = wgt[layer, blk, which, rows].astype(BF16)
-            else:
-                combine(step - 1, layer, blk, True)
-
-            w_one = wlo[layer, blk, 0]
-            w_two = wlo[layer, blk, 1]
+        @pl.loop(0, NB)
+        def _(blk):
+            combine(step - 1, layer, blk, True)
             for r in range(NR):
                 rows = pl.ds(r * RT, RT)
-                z = dot_nn(nlo[layer, rows], w_one)
-                pre[layer, blk, rows] = z
-                th = jnp.tanh(z * (GELU_C + (GELU_C * GELU_K) * (z * z)))
-                a_lo = (z * (0.5 + 0.5 * th)).astype(BF16)
-                act[layer, blk, rows] = a_lo
-                acc[rows] = acc[rows] + dot_nn(a_lo, w_two)
-
-        if first:
-            for blk in range(NB):
-                block(blk)
-        else:
-            pl.loop(0, NB)(block)
+                acc[rows] = acc[rows] + dot_nn(activation(layer, blk, rows), wlo[layer, blk, 1])
 
     def backward_layer(step, layer, send_now):
         if layer > 0:
@@ -222,7 +245,7 @@
             for r in range(NR):
                 rows = pl.ds(r * RT, RT)
                 u = dot_nt(elo[rows], w_two)
-                z = pre[layer, blk, rows]
+                z = dot_nn(nlo[layer, rows], w_one)
                 zz = z * z
                 th = jnp.tanh(z * (GELU_C + (GELU_C * GELU_K) * zz))
                 slope = (0.5 + 0.5 * th) * (1.0 + (z * (1.0 - th)) * (GELU_C + (3.0 * GELU_C * GELU_K) * zz))
@@ -236,28 +259,12 @@
             wire[layer, blk, 0] = q_one.astype(BF16)
             send_now(blk, 0)
 
-    def forward(step, first):
-        with jax.named_scope("fwd0"):
-            forward_layer(step, 0, first)
-        with jax.named_scope("fwd1"):
-            forward_layer(step, 1, first)
-
-    load_data(0, 0, 1).wait()
-    forward(0, True)
+    with jax.named_scope("fwd_first"):
+        first_forward()
     pl.semaphore_wait(barrier, n_rows + 1)
-
-    load_data(1, 0, 1).wait()
 
     @pl.loop(0, STEPS)
     def _(step):
-
-        @pl.loop(0, BATCH, step=128)
-        def _(r0):
-            rows = pl.ds(pl.multiple_of(r0, 128), 128)
-            e = (2.0 / (BATCH * DM)) * (acc[rows].astype(BF16).astype(F32) - tin[step, rows].astype(F32))
-            err[rows] = e
-            elo[rows] = e.astype(BF16)
-
         @pl.when(step > 0)
         def _():
             wait_sends()
@@ -286,7 +293,7 @@
         with jax.named_scope("bwd0"):
             backward_layer(step, 0, send_whole)
         for blk in range(EARLY, NB):
-            start_sends(step, 1, blk)
+            start_sends(step, 1, blk, hold=(1, blk) == SEND_ORDER[-1])
         with jax.named_scope("outward"):
             start_outward(step)
 
@@ -297,10 +304,15 @@
 
         @pl.when(step < STEPS - 1)
         def _():
-            forward(step + 1, False)
+            with jax.named_scope("fwd0"):
+                forward_layer(step + 1, 0)
+            with jax.named_scope("fwd1"):
+                forward_layer(step + 1, 1)
+            for r0 in range(0, BATCH, 128):
+                error(step + 1, pl.ds(r0, 128), acc[pl.ds(r0, 128)])
 
     for layer, blk in SEND_ORDER:
-        combine(STEPS - 1, layer, blk, False)
+        combine(STEPS - 1, layer, blk, False, held_back=(layer, blk) == SEND_ORDER[-1])
     wait_sends()
 
     @pl.when(inner)
@@ -342,7 +354,6 @@
                 pltpu.VMEM((BATCH, DM), F32),
                 pltpu.VMEM((BATCH, 128), F32),
                 pltpu.VMEM((LAYERS, NB, BATCH, FB), BF16),
-                pltpu.VMEM((LAYERS, NB, BATCH, FB), F32),
                 pltpu.VMEM((BATCH, DM), F32),
                 pltpu.VMEM((BATCH, DM), F32),
                 pltpu.VMEM((BATCH, DM), BF16),

time: 284 us -> 284 us (level)
  no operation moved by 1% of the time
where the time goes in v6:
time: 284 us
  Pallas kernels  283 us (100%)
    pallas_call x1, Pallas kernels, device_fn(): pl.pallas_call(functools.partial(kernel, n_rows, n_cols), out_shape=pltpu...  281 us

profile of v6, /device:TPU:0, one launch (start us, length us, event | category | flops | bytes accessed | tf_op | source)
XLA Modules:
  0.0 284.1 jit_solution(2741630484999974085)
XLA Ops:
  0.6 281.3 %shard_map.59.wgt = f32[2,4,2,256,256]{4,3,2,1,0:T(8,128)S(1)} custom-call(f32[2,256,1024]{2,1,0:T(8,128)} %bitcast.6, f32[2,1024,256]{2,1,0:T(8,128)} %bitcast.7, bf16[3,1024,256]{2,1,0:T(8,128)(2,1)} %bitcast.8, bf16[3,1024,256]{2,1,0:T(8,128)(2,1)} %bitcast.9), custom_call_target="tpu_custom_call" | custom-call | tf_op jit(solution)/shard_map/pallas_call | solution.py:342
  281.9 2.1 shard_map.60

commit v7 on v6

--- a/solution.py
+++ b/solution.py
@@ -166,7 +166,7 @@
                 tot = tot * 0.2
                 wgt[layer, blk, which, rows] = tot
                 if keep_lo:
-                    wlo[layer, blk, which, rows] = tot.astype(BF16)
+                    wlo[layer, blk, which, rows] = (tot if which else 0.5 * tot).astype(BF16)
 
     def normalise(layer, rows, x):
         inv = lax.rsqrt(jnp.mean(x * x, axis=-1, keepdims=True) + NORM_EPS)
@@ -177,11 +177,10 @@
             inv1[rows] = jnp.broadcast_to(inv, (x.shape[0], 128))
 
     def activation(layer, blk, rows):
-        z = dot_nn(nlo[layer, rows], wlo[layer, blk, 0])
-        th = jnp.tanh(z * (GELU_C + (GELU_C * GELU_K) * (z * z)))
-        a_lo = (z * (0.5 + 0.5 * th)).astype(BF16)
-        act[layer, blk, rows] = a_lo
-        return a_lo
+        half_z = dot_nn(nlo[layer, rows], wlo[layer, blk, 0])
+        th = jnp.tanh(half_z * (2.0 * GELU_C + (8.0 * GELU_C * GELU_K) * (half_z * half_z)))
+        act[layer, blk, rows] = (half_z * (1.0 + th)).astype(BF16)
+        return act[layer, blk, rows]
 
     def error(step, rows, total):
         e = (2.0 / (BATCH * DM)) * (total.astype(BF16).astype(F32) - tin[step, rows].astype(F32))
@@ -203,7 +202,8 @@
                 for blk in range(NB):
                     if r == 0:
                         loaded(layer, blk).wait()
-                        wlo[layer, blk] = wgt[layer, blk].astype(BF16)
+                        wlo[layer, blk, 0] = (0.5 * wgt[layer, blk, 0]).astype(BF16)
+                        wlo[layer, blk, 1] = wgt[layer, blk, 1].astype(BF16)
                     total = total + dot_nn(activation(layer, blk, rows), wlo[layer, blk, 1])
                 if layer == 0:
                     total = total.astype(BF16).astype(F32)
@@ -245,10 +245,10 @@
             for r in range(NR):
                 rows = pl.ds(r * RT, RT)
                 u = dot_nt(elo[rows], w_two)
-                z = dot_nn(nlo[layer, rows], w_one)
-                zz = z * z
-                th = jnp.tanh(z * (GELU_C + (GELU_C * GELU_K) * zz))
-                slope = (0.5 + 0.5 * th) * (1.0 + (z * (1.0 - th)) * (GELU_C + (3.0 * GELU_C * GELU_K) * zz))
+                half_z = dot_nn(nlo[layer, rows], w_one)
+                sq = half_z * half_z
+                th = jnp.tanh(half_z * (2.0 * GELU_C + (8.0 * GELU_C * GELU_K) * sq))
+                slope = (0.5 + 0.5 * th) * (1.0 + (half_z * (1.0 - th)) * (2.0 * GELU_C + (24.0 * GELU_C * GELU_K) * sq))
                 dz = (u * slope).astype(BF16)
                 dzb[rows] = dz
                 if layer > 0:
@@ -280,7 +280,7 @@
         @pl.loop(0, BATCH, step=128)
         def _(r0):
             rows = pl.ds(pl.multiple_of(r0, 128), 128)
-            m = macc[rows]
+            m = 2.0 * macc[rows]
             n = nf1[rows]
             inv = inv1[rows, 0:1]
             e = err[rows] + inv * (m - n * jnp.mean(m * n, axis=-1, keepdims=True))

time: 284 us -> 284 us (level)
  no operation moved by 1% of the time
where the time goes in v7:
time: 284 us
  Pallas kernels  283 us (100%)
    pallas_call x1, Pallas kernels, device_fn(): pl.pallas_call(functools.partial(kernel, n_rows, n_cols), out_shape=pltpu...  281 us

profile of v7, /device:TPU:0, one launch (start us, length us, event | category | flops | bytes accessed | tf_op | source)
XLA Modules:
  0.0 283.9 jit_solution(14885933307867511289)
XLA Ops:
  0.6 281.1 %shard_map.59.wgt = f32[2,4,2,256,256]{4,3,2,1,0:T(8,128)S(1)} custom-call(f32[2,256,1024]{2,1,0:T(8,128)} %bitcast.6, f32[2,1024,256]{2,1,0:T(8,128)} %bitcast.7, bf16[3,1024,256]{2,1,0:T(8,128)(2,1)} %bitcast.8, bf16[3,1024,256]{2,1,0:T(8,128)(2,1)} %bitcast.9), custom_call_target="tpu_custom_call" | custom-call | tf_op jit(solution)/shard_map/pallas_call | solution.py:342
  281.7 2.1 shard_map.60

commit v8 on v7

--- a/solution.py
+++ b/solution.py
@@ -21,7 +21,7 @@
 NB = DF // FB
 RT = 256
 NR = BATCH // RT
-RT1 = 256
+RT1 = 512
 MESH = pl.DeviceIdType.MESH
 F32 = jnp.float32
 BF16 = jnp.bfloat16
@@ -192,18 +192,22 @@
         for layer in range(LAYERS):
             if layer == LAYERS - 1:
                 load_data(1, 0, 1).wait()
+            if layer == 0:
+                for r0 in range(0, BATCH, 128):
+                    rows = pl.ds(r0, 128)
+                    normalise(layer, rows, ain[0, rows].astype(F32))
+            for blk in range(NB):
+                loaded(layer, blk).wait()
+            for blk in range(NB):
+                wlo[layer, blk, 0] = (0.5 * wgt[layer, blk, 0]).astype(BF16)
+                wlo[layer, blk, 1] = wgt[layer, blk, 1].astype(BF16)
             for r in range(BATCH // RT1):
                 rows = pl.ds(r * RT1, RT1)
                 if layer == 0:
                     total = ain[0, rows].astype(F32)
-                    normalise(layer, rows, total)
                 else:
                     total = acc[rows]
                 for blk in range(NB):
-                    if r == 0:
-                        loaded(layer, blk).wait()
-                        wlo[layer, blk, 0] = (0.5 * wgt[layer, blk, 0]).astype(BF16)
-                        wlo[layer, blk, 1] = wgt[layer, blk, 1].astype(BF16)
                     total = total + dot_nn(activation(layer, blk, rows), wlo[layer, blk, 1])
                 if layer == 0:
                     total = total.astype(BF16).astype(F32)

time: 284 us -> 283 us (level)
  no operation moved by 1% of the time
where the time goes in v8:
time: 283 us
  Pallas kernels  283 us (100%)
    pallas_call x1, Pallas kernels, device_fn(): pl.pallas_call(functools.partial(kernel, n_rows, n_cols), out_shape=pltpu...  280 us

profile of v8, /device:TPU:0, one launch (start us, length us, event | category | flops | bytes accessed | tf_op | source)
XLA Modules:
  0.0 283.2 jit_solution(3581193156626700233)
XLA Ops:
  0.6 280.5 %shard_map.59.wgt = f32[2,4,2,256,256]{4,3,2,1,0:T(8,128)S(1)} custom-call(f32[2,256,1024]{2,1,0:T(8,128)} %bitcast.6, f32[2,1024,256]{2,1,0:T(8,128)} %bitcast.7, bf16[3,1024,256]{2,1,0:T(8,128)(2,1)} %bitcast.8, bf16[3,1024,256]{2,1,0:T(8,128)(2,1)} %bitcast.9), custom_call_target="tpu_custom_call" | custom-call | tf_op jit(solution)/shard_map/pallas_call | solution.py:346
  281.1 2.1 shard_map.60
